TPU v7x, 32 devices: a whole 2x2x4 slice. The times are simulated.
32 devices in a mesh: dp: 4 (over y, x), cls: 8 (over z, core).
Axes of the slice: x: 2, y: 2, z: 4, core: 2. Of those that a mesh axis runs over, the one named last changes fastest.
Arguments:
- embeddings: float32 [2048, 512], P('dp'), may hold values from -60 to 60, as said below
- classifier: float32 [131072, 512], P(('dp', 'cls')), may hold values from -60 to 60, as said below
- labels: int32 [2048], replicated, may hold values from 0 to 131071
- row_scale: float32 [2048], replicated, may hold values from 16 to 512
Outputs:
- loss: float32 [2048], P(('dp', 'cls'))
Inputs may be any that keep to these rules, and one draw needn't show every extreme that they name: `embeddings`: rows of different scales. `classifier`: rows of different scales.
All inputs are finite; a program needn't handle non-finite values.
Results may differ from a plain program's by a relative error of at most 0.0003.
Values sent between devices are 32-bit elements; how exact they have to be, the bound alone decides.
A program may use at most 128 MiB of HBM per device.

v0:
```python
import functools
import math

import jax
import jax.numpy as jnp
from jax import lax
from jax.experimental import pallas as pl
from jax.experimental.pallas import tpu as pltpu
from jax.sharding import PartitionSpec as P

MARGIN = 0.5
COS_MARGIN = math.cos(MARGIN)
SIN_MARGIN = math.sin(MARGIN)
LOG2E = math.log2(math.e)
LN2 = math.log(2.0)
LOW = -1e30
MESH = pl.DeviceIdType.MESH


def kernel(ndp, ncls, chunk, emb_hbm, cls_hbm, lab_sm, lab_ref, scale_ref, out_ref,
           emb, raw, unit_w, picks, unit_e, buf0, buf1, stats, got,
           emb_sem, raw_sem, xs, xr, ys, yr, ds, dr, ss, sr):
    dp, cls = lax.axis_index("dp"), lax.axis_index("cls")
    core = lax.rem(cls, 2)
    ndev = ndp * ncls
    me = dp * ncls + cls
    rows, width = cls_hbm.shape
    half = width // 2
    piece = emb_hbm.shape[0] // 4
    groups, lanes = lab_ref.shape
    nchunk = rows // chunk
    offset = me * rows

    barrier = pltpu.get_barrier_semaphore()

    @pl.loop(1, ndev)
    def _(k):
        to = lax.rem(me + k, ndev)
        pl.semaphore_signal(barrier, inc=1, device_id=(to // ncls, lax.rem(to, ncls)), device_id_type=MESH)

    emb_in = [
        pltpu.make_async_copy(emb_hbm.at[:, pl.ds(c * half, half)], emb.at[0, c], emb_sem.at[c])
        for c in range(2)
    ]
    for copy in emb_in:
        copy.start()
    raw_in = [
        pltpu.make_async_copy(raw_hbm, raw.at[pl.ds(i * chunk, chunk)], raw_sem.at[i])
        for i in range(nchunk)
        for raw_hbm in [cls_hbm.at[pl.ds(i * chunk, chunk)]]
    ]
    for copy in raw_in:
        copy.start()

    def prepare(i):
        raw_in[i].wait()

        @pl.loop(0, chunk // 64)
        def _(b):
            at = pl.ds(pl.multiple_of(i * chunk + b * 64, 64), 64)
            w = raw[at, :]
            inv = lax.rsqrt(jnp.sum(w * w, axis=1, keepdims=True) + 1e-06)
            unit_w[at, :] = (w * inv).astype(jnp.bfloat16)

    early = nchunk // 2
    for i in range(early):
        prepare(i)
    for copy in emb_in:
        copy.wait()
    pl.semaphore_wait(barrier, ndev - 1)

    to_x = (dp ^ 1, cls)
    to_y = (dp ^ 2, cls)
    partner = (dp, cls ^ 1)

    def part(slot, j):
        return emb.at[slot, core, pl.ds(j * piece, piece)]

    def send(src, dst, s, r, k, to):
        copy = pltpu.make_async_remote_copy(
            src_ref=part(*src), dst_ref=part(*dst), send_sem=s.at[k], recv_sem=r.at[k],
            device_id=to, device_id_type=MESH,
        )
        copy.start()
        return copy

    x_slot = [(1, 0), (1, 1), (1, 2), (1, 3), (3, 2), (3, 3)]
    y_slot = [(2, 2), (2, 3), (2, 0), (2, 1), (3, 0), (3, 1)]
    x_copy, y_copy, d_copy = [], [], []
    for k in range(4):
        x_copy.append(send((0, x_slot[k][1]), x_slot[k], xs, xr, k, to_x))
        y_copy.append(send((0, y_slot[k][1]), y_slot[k], ys, yr, k, to_y))
    for i in range(early, nchunk):
        prepare(i)

    def forward(k):
        x_copy[k].wait_recv()
        y_copy[k].wait_recv()
        if k < 2:
            x_copy.append(send(y_slot[k], x_slot[k + 4], xs, xr, k + 4, to_x))
            y_copy.append(send(x_slot[k], y_slot[k + 4], ys, yr, k + 4, to_y))
        d_copy.append(send(x_slot[k], x_slot[k], ds, dr, 2 * k, partner))
        d_copy.append(send(y_slot[k], y_slot[k], ds, dr, 2 * k + 1, partner))

    def unit_rows(pair):
        left = jnp.concatenate([emb[s, 0, pl.ds(j * piece, piece), :] for s, j in pair], axis=0)
        right = jnp.concatenate([emb[s, 1, pl.ds(j * piece, piece), :] for s, j in pair], axis=0)
        values = jnp.concatenate([left, right], axis=1)
        return values * lax.rsqrt(jnp.sum(values * values, axis=1, keepdims=True) + 1e-06)

    wide = 2 * piece
    share = wide // nchunk

    def make_dot(pair, unit):
        group = [(dp ^ s) * 4 + j for s, j in pair]
        operand, picked = unit_e.at[unit % 2], picks.at[unit % 2]
        operand[...] = unit_rows(pair).astype(jnp.bfloat16)
        local = jnp.concatenate([lab_ref[pl.ds(g, 1), :] for g in group], axis=1) - offset
        scale = jnp.concatenate([scale_ref[pl.ds(g, 1), :] for g in group], axis=1)
        scale2 = scale * LOG2E

        def dot(i, buf):
            at = pl.ds(pl.multiple_of(i * chunk, chunk), chunk)
            cosine = lax.dot_general(
                unit_w[at, :], operand[...], (((1,), (1,)), ((), ())),
                preferred_element_type=jnp.float32,
            )
            ids = lax.broadcasted_iota(jnp.int32, (8, wide), 0)
            here = local - i * chunk
            top = None
            for r in range(0, chunk, 8):
                z = jnp.where(ids == here - r, LOW, cosine[r:r + 8, :] * scale2)
                buf[r:r + 8, :] = z
                top = z if top is None else jnp.maximum(top, z)
            first = i * share
            base = jnp.where(first < piece, group[0] * piece, group[1] * piece - piece) + first
            for t in range(0, share, 16):
                found = [raw[pl.ds(lab_sm[base + t + n], 1), :] for n in range(16)]
                for n in range(16):
                    picked[i, t + n:t + n + 1, :] = found[n]
            return top

        return dot, group, local, scale, picked

    def fold(buf, top, peak, total):
        fresh = jnp.maximum(peak, top)
        parts = [total * jnp.exp2(peak - fresh)]
        for r in range(0, chunk, 8):
            term = jnp.exp2(buf[r:r + 8, :] - fresh)
            if len(parts) < 4:
                parts.append(term)
            else:
                n = (r // 8) % 4
                parts[n] = parts[n] + term
        return fresh, (parts[0] + parts[1]) + (parts[2] + parts[3])

    def finish(pair, unit, best, total, group, local, scale, picked):
        units = unit_rows(pair)
        rows_f = picked[...].reshape(wide, -1)
        rows_f = rows_f * lax.rsqrt(jnp.sum(rows_f * rows_f, axis=1, keepdims=True) + 1e-06)
        cosine = jnp.sum(units * rows_f, axis=1, keepdims=True)
        across = units - cosine * rows_f
        sine = jnp.sqrt(jnp.sum(across * across, axis=1, keepdims=True))
        target = cosine * COS_MARGIN - sine * SIN_MARGIN
        target = jnp.transpose(jnp.broadcast_to(target, (wide, 128)))[0:1, :]
        owned = (local >= 0) & (local < rows)
        target = jnp.where(owned, scale * target, 0.0)
        for n, g in enumerate(group):
            cut = slice(n * piece, (n + 1) * piece)
            stats[pl.ds(g, 1), 0:1, :] = best[:, cut][None]
            stats[pl.ds(g, 1), 1:2, :] = total[:, cut][None]
            stats[pl.ds(g, 1), 2:3, :] = target[:, cut][None]

    pairs = [[(0, 0), (0, 1)], [(0, 2), (0, 3)]] + [[x_slot[k], y_slot[k]] for k in range(6)]

    def ready(unit):
        if 1 <= unit <= 6:
            forward(unit - 1)
        if unit >= 2:
            d_copy[2 * unit - 4].wait_recv()
            d_copy[2 * unit - 3].wait_recv()

    ready(0)
    made = make_dot(pairs[0], 0)
    top = made[0](0, buf0)
    for unit in range(8):
        dot, rest_of = made[0], made[1:]

        def both(h, carry, dot=dot):
            top, peak, total = carry
            i = 2 * h
            after = dot(i + 1, buf1)
            peak, total = fold(buf0, top, peak, total)
            top = dot(i + 2, buf0)
            return (top,) + fold(buf1, after, peak, total)

        start = (top, jnp.full((8, wide), LOW, jnp.float32), jnp.zeros((8, wide), jnp.float32))
        top, peak, total = lax.fori_loop(0, nchunk // 2 - 1, both, start)
        after = dot(nchunk - 1, buf1)
        peak, total = fold(buf0, top, peak, total)
        if unit < 7:
            ready(unit + 1)
            made = make_dot(pairs[unit + 1], unit + 1)
            top = made[0](0, buf0)
        peak, total = fold(buf1, after, peak, total)
        best = jnp.max(peak, axis=0, keepdims=True)
        total = jnp.sum(total * jnp.exp2(peak - best), axis=0, keepdims=True)
        finish(pairs[unit], unit, best, total, *rest_of)

    share = groups * lanes // ndev
    per = lanes // share

    def outgoing(k):
        to = lax.rem(me + k, ndev)
        return pltpu.make_async_remote_copy(
            src_ref=stats.at[to // per], dst_ref=got.at[k], send_sem=ss, recv_sem=sr,
            device_id=(to // ncls, lax.rem(to, ncls)), device_id_type=MESH,
        )

    @pl.loop(1, ndev)
    def _(k):
        outgoing(k).start()

    got[0] = stats[me // per]
    for copy in x_copy + y_copy + d_copy:
        copy.wait_send()
    rest = got.at[pl.ds(1, ndev - 1)]
    pltpu.make_async_copy(rest, rest, ss).wait()
    pltpu.make_async_copy(rest, rest, sr).wait()

    everyone = got[...]
    peaks, totals = everyone[:, 0, :], everyone[:, 1, :]
    target = jnp.sum(everyone[:, 2, :], axis=0, keepdims=True)
    best = jnp.maximum(jnp.max(peaks, axis=0, keepdims=True), target * LOG2E)
    total = jnp.sum(totals * jnp.exp2(peaks - best), axis=0, keepdims=True) + jnp.exp2(target * LOG2E - best)
    loss = best * LN2 + jnp.log(total) - target
    mine = loss[:, 0:share]
    for q in range(1, per):
        mine = jnp.where(lax.rem(me, per) == q, loss[:, q * share:(q + 1) * share], mine)
    out_ref[...] = mine


def body(embeddings, classifier, labels, row_scale):
    ndp, ncls = lax.axis_size("dp"), lax.axis_size("cls")
    assert ndp == 4 and ncls % 2 == 0
    ndev = ndp * ncls
    block, width = embeddings.shape
    rows = classifier.shape[0]
    count = labels.shape[0]
    piece = block // 4
    chunk = rows // 8
    groups = count // piece
    offset = lax.axis_index(("dp", "cls")) * rows
    nearest = jnp.clip(labels - offset, 0, rows - 1)
    f32 = jnp.float32
    any_spec = pl.BlockSpec(memory_space=pl.ANY)
    vmem = pl.BlockSpec(memory_space=pltpu.VMEM)
    dma = pltpu.SemaphoreType.DMA
    out = pl.pallas_call(
        functools.partial(kernel, ndp, ncls, chunk),
        out_shape=jax.ShapeDtypeStruct((1, count // ndev), f32),
        in_specs=[any_spec, any_spec, pl.BlockSpec(memory_space=pltpu.SMEM), vmem, vmem],
        out_specs=vmem,
        scratch_shapes=[
            pltpu.VMEM((4, 2, block, width // 2), f32),
            pltpu.VMEM((rows, width), f32),
            pltpu.VMEM((rows, width), jnp.bfloat16),
            pltpu.VMEM((2, 8, 2 * piece // 8, width), f32),
            pltpu.VMEM((2, 2 * piece, width), jnp.bfloat16),
            pltpu.VMEM((chunk, 2 * piece), f32),
            pltpu.VMEM((chunk, 2 * piece), f32),
            pltpu.VMEM((groups, 8, piece), f32),
            pltpu.VMEM((ndev, 8, piece), f32),
            dma((2,)), dma((8,)), dma((6,)), dma((6,)), dma((6,)), dma((6,)),
            dma((12,)), dma((12,)), dma, dma,
        ],
        compiler_params=pltpu.CompilerParams(
            collective_id=0, has_side_effects=True, vmem_limit_bytes=56 * 1024 * 1024
        ),
    )(embeddings, classifier, nearest, labels.reshape(groups, piece), row_scale.reshape(groups, piece))
    return out.reshape(count // ndev)


def solution(mesh):
    placed = (P("dp", None), P(("dp", "cls"), None), P(), P())
    return jax.shard_map(
        body, mesh=mesh, in_specs=placed, out_specs=P(("dp", "cls")), check_vma=False
    )
```

profile of v0, /device:TPU:0, one launch (start us, length us, event | category | flops | bytes accessed | tf_op | source)
XLA Modules:
  0.0 45.5 jit_solution(1014914288614349267)
XLA Ops:
  0.0 1.3 %subtract_clamp_fusion.lab_sm = s32[2048]{0:T(1024)} fusion(s32[2048]{0:T(1024)} %param.6, s32[]{:T(128)S(6)} %mul.7), kind=kLoop, calls=%fused_computation | loop fusion | flops 4096 | bytes 16388 | tf_op jit(solution)/shard_map/jit(clip)/min | solution.py:254
  1.3 43.0 %shard_map.46 = f32[1,64]{1,0:T(1,128)} custom-call(f32[512,512]{1,0:T(8,128)} %emb_hbm.1, f32[4096,512]{1,0:T(8,128)} %cls_hbm.1, s32[2048]{0:T(1024)} %subtract_clamp_fusion.lab_sm, s32[16,128]{1,0:T(8,128)} %bitcast.3, f32[16,128]{1,0:T(8,128)} %bitcast.4), custom_call_target="tpu_custom_call" | custom-call | tf_op jit(solution)/shard_map/pallas_call | solution.py:259
  44.3 1.1 %copy.6 = f32[64]{0:T(128)} copy(f32[64]{0:T(128)} %bitcast.5) | data formatting | bytes 512
where the time goes:
time: 45.8 us; the launch traced here: 45.5 us
  Pallas kernels  43 us (94%)
  other arithmetic  1.29 us (3%)
  local copies, waits for them, and re-layouts  1.11 us (2%)
    pallas_call x1, Pallas kernels, body(): pl.pallas_call(functools.partial(kernel, ndp, ncls, chunk), out_shape=jax...  43 us
    min x1, other arithmetic, body(): nearest = jnp.clip(labels - offset, 0, rows - 1)  1.29 us
    unnamed x1, local copies, waits for them, and re-layouts  1.11 us

commit v1 on v0

v1 whole, which is shorter than its diff:
```python
import functools
import math

import jax
import jax.numpy as jnp
from jax import lax
from jax.experimental import pallas as pl
from jax.experimental.pallas import tpu as pltpu
from jax.sharding import PartitionSpec as P

MARGIN = 0.5
COS_MARGIN = math.cos(MARGIN)
SIN_MARGIN = math.sin(MARGIN)
LOG2E = math.log2(math.e)
LN2 = math.log(2.0)
LOW = -1e30
MESH = pl.DeviceIdType.MESH


def kernel(ndp, ncls, chunk, emb_hbm, cls_hbm, lab_sm, lab_ref, scale_ref, out_ref,
           emb, raw, unit_w, picks, unit_e, inv_e, stats, got,
           emb_sem, raw_sem, xs, xr, ys, yr, ds, dr, ss, sr):
    dp, cls = lax.axis_index("dp"), lax.axis_index("cls")
    core = lax.rem(cls, 2)
    ndev = ndp * ncls
    me = dp * ncls + cls
    rows, width = cls_hbm.shape
    half = width // 2
    piece = emb_hbm.shape[0] // 4
    groups, lanes = lab_ref.shape
    nchunk = rows // chunk
    offset = me * rows

    barrier = pltpu.get_barrier_semaphore()

    @pl.loop(1, ndev)
    def _(k):
        to = lax.rem(me + k, ndev)
        pl.semaphore_signal(barrier, inc=1, device_id=(to // ncls, lax.rem(to, ncls)), device_id_type=MESH)

    emb_in = [
        pltpu.make_async_copy(emb_hbm.at[:, pl.ds(c * half, half)], emb.at[0, c], emb_sem.at[c])
        for c in range(2)
    ]
    for copy in emb_in:
        copy.start()
    raw_in = [
        pltpu.make_async_copy(raw_hbm, raw.at[pl.ds(i * chunk, chunk)], raw_sem.at[i])
        for i in range(nchunk)
        for raw_hbm in [cls_hbm.at[pl.ds(i * chunk, chunk)]]
    ]
    for copy in raw_in:
        copy.start()

    def prepare(i):
        raw_in[i].wait()

        @pl.loop(0, chunk // 256)
        def _(b):
            at = pl.ds(pl.multiple_of(i * chunk + b * 256, 256), 256)
            w = raw[at, :]
            inv = lax.rsqrt(jnp.sum(w * w, axis=1, keepdims=True) + 1e-06)
            unit_w[at, :] = (w * inv).astype(jnp.bfloat16)

    early = nchunk // 2
    for i in range(early):
        prepare(i)
    for copy in emb_in:
        copy.wait()
    pl.semaphore_wait(barrier, ndev - 1)

    to_x = (dp ^ 1, cls)
    to_y = (dp ^ 2, cls)
    partner = (dp, cls ^ 1)

    def part(slot, j):
        return emb.at[slot, core, pl.ds(j * piece, piece)]

    def send(src, dst, s, r, k, to):
        copy = pltpu.make_async_remote_copy(
            src_ref=part(*src), dst_ref=part(*dst), send_sem=s.at[k], recv_sem=r.at[k],
            device_id=to, device_id_type=MESH,
        )
        copy.start()
        return copy

    x_slot = [(1, 0), (1, 1), (1, 2), (1, 3), (3, 2), (3, 3)]
    y_slot = [(2, 2), (2, 3), (2, 0), (2, 1), (3, 0), (3, 1)]
    x_copy, y_copy, d_copy = [], [], []
    for k in range(4):
        x_copy.append(send((0, x_slot[k][1]), x_slot[k], xs, xr, k, to_x))
        y_copy.append(send((0, y_slot[k][1]), y_slot[k], ys, yr, k, to_y))
    for i in range(early, nchunk):
        prepare(i)

    def forward(k):
        x_copy[k].wait_recv()
        y_copy[k].wait_recv()
        if k < 2:
            x_copy.append(send(y_slot[k], x_slot[k + 4], xs, xr, k + 4, to_x))
            y_copy.append(send(x_slot[k], y_slot[k + 4], ys, yr, k + 4, to_y))
        d_copy.append(send(x_slot[k], x_slot[k], ds, dr, 2 * k, partner))
        d_copy.append(send(y_slot[k], y_slot[k], ds, dr, 2 * k + 1, partner))

    wide = 2 * piece
    tall = rows // 2
    group_rows = 64
    share = wide * group_rows // rows
    ids = lax.broadcasted_iota(jnp.int32, (8, wide), 0)

    def tree(parts, op):
        while len(parts) > 1:
            parts = [op(*parts[k:k + 2]) if k + 1 < len(parts) else parts[k] for k in range(0, len(parts), 2)]
        return parts[0]

    def down(row):
        return jnp.transpose(jnp.broadcast_to(row, (piece, lanes)))

    def halves(s, j):
        at = pl.ds(j * piece, piece)
        return jnp.concatenate([emb[s, 0, at, :], emb[s, 1, at, :]], axis=1)

    def quarters(values, factor):
        return [values[:, q:q + lanes] * factor for q in range(0, width, lanes)]

    def row_sum(parts):
        return jnp.sum(tree(parts, jnp.add), axis=1, keepdims=True)

    def load_unit(pair):
        for n, (s, j) in enumerate(pair):
            values = halves(s, j)
            inv = lax.rsqrt(jnp.sum(values * values, axis=1, keepdims=True) + 1e-06)
            inv_e[n * piece:(n + 1) * piece, :] = jnp.broadcast_to(inv, (piece, lanes))
            factor = down(scale_ref[pl.ds((dp ^ s) * 4 + j, 1), :] * LOG2E) * inv
            unit_e[n * piece:(n + 1) * piece, :] = jnp.concatenate(
                [v.astype(jnp.bfloat16) for v in quarters(values, factor)], axis=1)

    def sweep(pair):
        group = [(dp ^ s) * 4 + j for s, j in pair]
        local = jnp.concatenate([lab_ref[pl.ds(g, 1), :] for g in group], axis=1) - offset
        below = local - ids

        def step(i, carry):
            peak, total = carry
            logits = lax.dot_general(
                unit_w[pl.ds(pl.multiple_of(i * tall, tall), tall), :], unit_e[...], (((1,), (1,)), ((), ())),
                preferred_element_type=jnp.float32,
            )
            here = below - i * tall
            first = i * piece
            base = jnp.where(i == 0, group[0], group[1]) * piece
            for g in range(0, tall, group_rows):
                z = [jnp.where(here == r, LOW, logits[r:r + 8, :]) for r in range(g, g + group_rows, 8)]
                fresh = jnp.maximum(peak, tree(z, jnp.maximum))
                terms = [jnp.exp2(t - fresh) for t in z] + [total * jnp.exp2(peak - fresh)]
                peak, total = fresh, tree(terms, jnp.add)
                t = g // group_rows * share
                for n in range(t, t + share):
                    row = lax.rem(lab_sm[base + n], rows) if rows & (rows - 1) else lab_sm[base + n] & (rows - 1)
                    picks[pl.ds(first + n, 1), :] = raw[pl.ds(row, 1), :]
            return peak, total

        start = (jnp.full((8, wide), LOW, jnp.float32), jnp.zeros((8, wide), jnp.float32))
        peak, total = lax.fori_loop(0, 2, step, start)
        best = jnp.max(peak, axis=0, keepdims=True)
        total = jnp.sum(total * jnp.exp2(peak - best), axis=0, keepdims=True)
        for n, g in enumerate(group):
            cut = slice(n * piece, (n + 1) * piece)
            stats[pl.ds(g, 1), 0:1, :] = best[:, cut][None]
            stats[pl.ds(g, 1), 1:2, :] = total[:, cut][None]

    def finish(pair):
        for n, (s, j) in enumerate(pair):
            g = (dp ^ s) * 4 + j
            at = slice(n * piece, (n + 1) * piece)
            units = quarters(halves(s, j), inv_e[at, :])
            picked = picks[at, :]
            inv = lax.rsqrt(jnp.sum(picked * picked, axis=1, keepdims=True) + 1e-06)
            picked = quarters(picked, inv)
            cosine = row_sum([u * p for u, p in zip(units, picked)])
            across = [u - cosine * p for u, p in zip(units, picked)]
            sine = jnp.sqrt(row_sum([v * v for v in across]))
            target = cosine * COS_MARGIN - sine * SIN_MARGIN
            target = jnp.transpose(jnp.broadcast_to(target, (piece, lanes)))[0:1, :]
            local = lab_ref[pl.ds(g, 1), :] - offset
            owned = (local >= 0) & (local < rows)
            stats[pl.ds(g, 1), 2:3, :] = jnp.where(owned, scale_ref[pl.ds(g, 1), :] * target, 0.0)[None]

    pairs = [[(0, 0), (0, 1)], [(0, 2), (0, 3)]] + [[x_slot[k], y_slot[k]] for k in range(6)]

    def ready(unit):
        if 1 <= unit <= 6:
            forward(unit - 1)
        if unit >= 2:
            d_copy[2 * unit - 4].wait_recv()
            d_copy[2 * unit - 3].wait_recv()

    for unit in range(8):
        ready(unit)
        load_unit(pairs[unit])
        sweep(pairs[unit])
        finish(pairs[unit])

    share = groups * lanes // ndev
    per = lanes // share

    def outgoing(k):
        to = lax.rem(me + k, ndev)
        return pltpu.make_async_remote_copy(
            src_ref=stats.at[to // per], dst_ref=got.at[k], send_sem=ss, recv_sem=sr,
            device_id=(to // ncls, lax.rem(to, ncls)), device_id_type=MESH,
        )

    @pl.loop(1, ndev)
    def _(k):
        outgoing(k).start()

    got[0] = stats[me // per]
    for copy in x_copy + y_copy + d_copy:
        copy.wait_send()
    rest = got.at[pl.ds(1, ndev - 1)]
    pltpu.make_async_copy(rest, rest, ss).wait()
    pltpu.make_async_copy(rest, rest, sr).wait()

    everyone = got[...]
    peaks, totals = everyone[:, 0, :], everyone[:, 1, :]
    target = jnp.sum(everyone[:, 2, :], axis=0, keepdims=True)
    best = jnp.maximum(jnp.max(peaks, axis=0, keepdims=True), target * LOG2E)
    total = jnp.sum(totals * jnp.exp2(peaks - best), axis=0, keepdims=True) + jnp.exp2(target * LOG2E - best)
    loss = best * LN2 + jnp.log(total) - target
    mine = loss[:, 0:share]
    for q in range(1, per):
        mine = jnp.where(lax.rem(me, per) == q, loss[:, q * share:(q + 1) * share], mine)
    out_ref[...] = mine


def body(embeddings, classifier, labels, row_scale):
    ndp, ncls = lax.axis_size("dp"), lax.axis_size("cls")
    assert ndp == 4 and ncls % 2 == 0
    ndev = ndp * ncls
    block, width = embeddings.shape
    rows = classifier.shape[0]
    count = labels.shape[0]
    piece = block // 4
    chunk = rows // 8
    groups = count // piece
    f32 = jnp.float32
    any_spec = pl.BlockSpec(memory_space=pl.ANY)
    vmem = pl.BlockSpec(memory_space=pltpu.VMEM)
    dma = pltpu.SemaphoreType.DMA
    out = pl.pallas_call(
        functools.partial(kernel, ndp, ncls, chunk),
        out_shape=jax.ShapeDtypeStruct((1, count // ndev), f32),
        in_specs=[any_spec, any_spec, pl.BlockSpec(memory_space=pltpu.SMEM), vmem, vmem],
        out_specs=vmem,
        scratch_shapes=[
            pltpu.VMEM((4, 2, block, width // 2), f32),
            pltpu.VMEM((rows, width), f32),
            pltpu.VMEM((rows, width), jnp.bfloat16),
            pltpu.VMEM((2 * piece, width), f32),
            pltpu.VMEM((2 * piece, width), jnp.bfloat16),
            pltpu.VMEM((2 * piece, 128), f32),
            pltpu.VMEM((groups, 8, piece), f32),
            pltpu.VMEM((ndev, 8, piece), f32),
            dma((2,)), dma((8,)), dma((6,)), dma((6,)), dma((6,)), dma((6,)),
            dma((12,)), dma((12,)), dma, dma,
        ],
        compiler_params=pltpu.CompilerParams(
            collective_id=0, has_side_effects=True, vmem_limit_bytes=56 * 1024 * 1024
        ),
    )(embeddings, classifier, labels, labels.reshape(groups, piece), row_scale.reshape(groups, piece))
    return out.reshape(count // ndev)


def solution(mesh):
    placed = (P("dp", None), P(("dp", "cls"), None), P(), P())
    return jax.shard_map(
        body, mesh=mesh, in_specs=placed, out_specs=P(("dp", "cls")), check_vma=False
    )
```

time: 45.8 us -> 39.2 us (0.86)
  Pallas kernels: 43 us -> 37.7 us
  other arithmetic: 1.29 us -> 0 us
    pallas_call x1, Pallas kernels: 43 us -> 37.7 us  [body(): pl.pallas_call(functools.partial(kernel, ndp, ncls, chunk), out_shape=jax...]
    min x1 -> x0, other arithmetic: 1.29 us -> none  [body(): nearest = jnp.clip(labels - offset, 0, rows - 1)]
where the time goes in v1:
time: 39.2 us; the launch traced here: 38.9 us
  Pallas kernels  37.7 us (96%)
  local copies, waits for them, and re-layouts  1.19 us (3%)
    pallas_call x1, Pallas kernels, body(): pl.pallas_call(functools.partial(kernel, ndp, ncls, chunk), out_shape=jax...  37.7 us
    unnamed x1, local copies, waits for them, and re-layouts  1.19 us

profile of v1, /device:TPU:0, one launch (start us, length us, event | category | flops | bytes accessed | tf_op | source)
XLA Modules:
  0.0 38.9 jit_solution(12226131146768718410)
XLA Ops:
  0.0 37.7 %shard_map.46 = f32[1,64]{1,0:T(1,128)} custom-call(f32[512,512]{1,0:T(8,128)} %emb_hbm.1, f32[4096,512]{1,0:T(8,128)} %cls_hbm.1, s32[2048]{0:T(1024)} %lab_sm.1, s32[16,128]{1,0:T(8,128)} %bitcast.3, f32[16,128]{1,0:T(8,128)} %bitcast.4), custom_call_target="tpu_custom_call" | custom-call | tf_op jit(solution)/shard_map/pallas_call | solution.py:251
  37.7 1.2 %copy.6 = f32[64]{0:T(128)} copy(f32[64]{0:T(128)} %bitcast.5) | data formatting | bytes 512

commit v2 on v1

v2 whole, which is shorter than its diff:
```python
import functools
import math

import jax
import jax.numpy as jnp
from jax import lax
from jax.experimental import pallas as pl
from jax.experimental.pallas import tpu as pltpu
from jax.sharding import PartitionSpec as P

MARGIN = 0.5
COS_MARGIN = math.cos(MARGIN)
SIN_MARGIN = math.sin(MARGIN)
LOG2E = math.log2(math.e)
LN2 = math.log(2.0)
LOW = -1e30
MESH = pl.DeviceIdType.MESH
F, N = 0, 1


def tree(parts, op):
    while len(parts) > 1:
        parts = [op(*parts[k:k + 2]) if k + 1 < len(parts) else parts[k] for k in range(0, len(parts), 2)]
    return parts[0]


def kernel(ndp, ncls, chunk, emb_hbm, cls_hbm, lab_sm, lab_ref, scale_ref, out_ref,
           emb, raw, unit_w, picks, unit_e, inv_e, stats, got,
           emb_sem, raw_sem, xs, xr, ys, yr, zs, zr, ds, dr, ss, sr):
    dp, cls = lax.axis_index("dp"), lax.axis_index("cls")
    core = lax.rem(cls, 2)
    ndev = ndp * ncls
    me = dp * ncls + cls
    rows, width = cls_hbm.shape
    piece = emb_hbm.shape[0] // 8
    part = piece // 2
    groups, lanes = lab_ref.shape
    nchunk = rows // chunk
    offset = me * rows
    share = groups * lanes // ndev

    emb_in = pltpu.make_async_copy(emb_hbm, emb.at[0], emb_sem)
    emb_in.start()
    barrier = pltpu.get_barrier_semaphore()

    @pl.loop(1, ndev)
    def _(k):
        to = lax.rem(me + k, ndev)
        pl.semaphore_signal(barrier, inc=1, device_id=(to // ncls, lax.rem(to, ncls)), device_id_type=MESH)

    raw_in = [
        pltpu.make_async_copy(cls_hbm.at[pl.ds(i * chunk, chunk)], raw.at[pl.ds(i * chunk, chunk)], raw_sem.at[i])
        for i in range(nchunk)
    ]
    for copy in raw_in:
        copy.start()
    emb_in.wait()
    pl.semaphore_wait(barrier, ndev - 1)

    to_x = (dp ^ 1, cls)
    to_y = (dp ^ 2, cls)
    to_z = (dp, cls ^ 2)
    partner = (dp, cls ^ 1)
    near = cls * share // (4 * piece) * 4
    starts = (4 - near, near)
    turn = lax.rem(cls // 2, 2) * 2
    sx = (0, turn)
    sy = (2, -turn)

    def place(half, index):
        base, shift = index
        return starts[half] + base + shift

    def at(index, by):
        return (index[0] + by, index[1])

    def own(slot, p):
        return emb.at[slot, pl.ds(p * piece + core * part, part)]

    def send(source, slot, p, s, r, k, to):
        copy = pltpu.make_async_remote_copy(
            src_ref=own(source, p), dst_ref=own(slot, p), send_sem=s.at[k], recv_sem=r.at[k],
            device_id=to, device_id_type=MESH,
        )
        copy.start()
        return copy

    x_plan = [(1, F, sx), (1, F, at(sx, 1)), (1, N, sx), (1, N, at(sx, 1)), (3, F, sy), (3, F, at(sy, 1)),
              (1, N, at(sy, 1)), (3, N, sy), (3, N, at(sy, 1))]
    y_plan = [(2, F, at(sy, 1)), (2, F, sy), (2, N, at(sy, 1)), (2, N, sy), (3, F, at(sx, 1)), (3, F, sx),
              (2, N, sx), (3, N, at(sx, 1)), (3, N, sx)]
    z_plan = [(1, F, sx), (2, F, at(sy, 1)), (1, F, at(sx, 1)), (2, F, sy), (1, N, sx), (2, N, at(sy, 1))]

    def other(index):
        return (2 - index[0] if index[0] % 2 == 0 else 4 - index[0], -index[1])

    came_z = [(slot, half, other(index)) for slot, half, index in z_plan]

    def remote(spot, source, s, r, k, to):
        slot, half, index = spot
        p = place(half, index)
        return pltpu.make_async_remote_copy(
            src_ref=own(source, p), dst_ref=own(slot, p), send_sem=s.at[k], recv_sem=r.at[k],
            device_id=to, device_id_type=MESH,
        )

    def x_copy(k):
        return remote(x_plan[k], 0 if x_plan[k][0] == 1 else 2, xs, xr, k, to_x)

    def y_copy(k):
        return remote(y_plan[k], 0 if y_plan[k][0] == 2 else 1, ys, yr, k, to_y)

    def z_copy(k):
        return remote(z_plan[k], z_plan[k][0], zs, zr, k, to_z)

    def d_copy(k):
        copy, plan, n = d_order[k]
        return remote(plan[n], plan[n][0], ds, dr, k, partner)

    X, Y, Z = (x_copy, x_plan), (y_copy, y_plan), (z_copy, came_z)
    arrivals = [
        [(*X, 0), (*Y, 0)],
        [(*X, 1), (*Y, 1)],
        [(*X, 2), (*Y, 2), (*X, 3), (*Y, 3)],
        [(*Z, 0), (*Z, 1), (*X, 4), (*Y, 4)],
        [(*Z, 2), (*X, 5), (*Y, 5), (*Z, 3)],
        [(*X, 6), (*Y, 6), (*Z, 4), (*Z, 5)],
        [(*X, 7), (*Y, 7), (*X, 8), (*Y, 8)],
    ]
    relays = [
        [(z_copy, 0), (z_copy, 1)],
        [(x_copy, 4), (y_copy, 4), (z_copy, 2), (z_copy, 3), (x_copy, 5), (y_copy, 5), (x_copy, 6), (y_copy, 6)],
        [(z_copy, 4), (z_copy, 5), (x_copy, 7), (y_copy, 7), (x_copy, 8), (y_copy, 8)],
        [], [], [], [],
    ]
    d_order = [entry for step in arrivals for entry in step]

    def forward(step):
        done = sum(len(group) for group in arrivals[:step])
        for n, (copy, _, k) in enumerate(arrivals[step]):
            copy(k).wait_recv()
            d_copy(done + n).start()
        for copy, k in relays[step]:
            copy(k).start()

    for k in range(4):
        x_copy(k).start()
        y_copy(k).start()

    def prepare(i):
        raw_in[i].wait()

        @pl.loop(0, chunk // 256)
        def _(b):
            rows_at = pl.ds(pl.multiple_of(i * chunk + b * 256, 256), 256)
            w = raw[rows_at, :]
            inv = lax.rsqrt(jnp.sum(w * w, axis=1, keepdims=True) + 1e-06)
            unit_w[rows_at, :] = (w * inv).astype(jnp.bfloat16)

    for i in range(nchunk):
        prepare(i)

    zx, zy = sy, sx
    units = [
        [(0, F, (0, 0)), (0, F, (1, 0)), (0, F, (2, 0)), (0, F, (3, 0))],
        [(0, N, (0, 0)), (0, N, (1, 0)), (0, N, (2, 0)), (0, N, (3, 0))],
        [(1, F, sx), (1, F, at(sx, 1)), (2, F, sy), (2, F, at(sy, 1))],
        [(1, N, sx), (1, N, at(sx, 1)), (2, N, sy), (2, N, at(sy, 1))],
        [(1, F, zx), (2, F, at(zy, 1)), (3, F, sy), (3, F, at(sx, 1))],
        [(3, F, sx), (3, F, at(sy, 1)), (2, F, zy), (1, F, at(zx, 1))],
        [(2, N, sx), (1, N, at(sy, 1)), (1, N, zx), (2, N, at(zy, 1))],
        [(3, N, sy), (3, N, at(sy, 1)), (3, N, sx), (3, N, at(sx, 1))],
    ]
    wide = 4 * piece
    tall = rows // 2
    group_rows = 64
    ids = lax.broadcasted_iota(jnp.int32, (8, wide), 0)
    first_half = lax.broadcasted_iota(jnp.int32, (1, lanes), 1) < piece

    def where_of(spot):
        slot, half, index = spot
        return slot, dp ^ slot, place(half, index)

    def row_of(ref, pair):
        both = []
        for spot in pair:
            _, block, p = where_of(spot)
            both.append(ref[pl.ds(block * 4 + p // 2, 1), :])
        return jnp.where(first_half, both[0], both[1])

    def values_of(pair):
        both = []
        for spot in pair:
            slot, _, p = where_of(spot)
            both.append(emb[slot, pl.ds(pl.multiple_of(p * piece, piece), piece), :])
        return jnp.concatenate(both, axis=0)

    def quarters(values, factor):
        return [values[:, q:q + lanes] * factor for q in range(0, width, lanes)]

    def row_sum(parts):
        return jnp.sum(tree(parts, jnp.add), axis=1, keepdims=True)

    def flip(values):
        return jnp.transpose(jnp.broadcast_to(values, (lanes, lanes)))

    def load_unit(unit):
        for n in range(2):
            pair = unit[2 * n:2 * n + 2]
            values = values_of(pair)
            inv = lax.rsqrt(jnp.sum(values * values, axis=1, keepdims=True) + 1e-06)
            rows_at = slice(n * lanes, (n + 1) * lanes)
            inv_e[rows_at, :] = jnp.broadcast_to(inv, (lanes, lanes))
            factor = flip(row_of(scale_ref, pair) * LOG2E) * inv
            unit_e[rows_at, :] = jnp.concatenate(
                [v.astype(jnp.bfloat16) for v in quarters(values, factor)], axis=1)

    def sweep(unit, below, hook):
        bases = []
        for spot in unit:
            _, block, p = where_of(spot)
            bases.append((block * 8 + p) * piece)
        count = lanes * group_rows // tall

        def step(i, carry):
            peak, total = carry
            logits = lax.dot_general(
                unit_w[pl.ds(pl.multiple_of(i * tall, tall), tall), :], unit_e[...], (((1,), (1,)), ((), ())),
                preferred_element_type=jnp.float32,
            )
            here = below - i * tall
            base = [jnp.where(i == 0, bases[k], bases[2 + k]) for k in range(2)]
            for g in range(0, tall, group_rows):
                z = [jnp.where(here == r, LOW, logits[r:r + 8, :]) for r in range(g, g + group_rows, 8)]
                fresh = jnp.maximum(peak, tree(z, jnp.maximum))
                terms = [jnp.exp2(t - fresh) for t in z] + [total * jnp.exp2(peak - fresh)]
                peak, total = fresh, tree(terms, jnp.add)
                t = g // group_rows * count
                for n in range(t, t + count):
                    label = lab_sm[base[n // piece] + n % piece]
                    row = lax.rem(label, rows) if rows & (rows - 1) else label & (rows - 1)
                    picks[pl.ds(i * lanes + n, 1), :] = raw[pl.ds(row, 1), :]
            if hook is not None:
                pl.when(i == 0)(lambda: forward(hook))
            return peak, total

        start = (jnp.full((8, wide), LOW, jnp.float32), jnp.zeros((8, wide), jnp.float32))
        return lax.fori_loop(0, 2, step, start)

    def finish(number, unit, local, peak, total):
        best = jnp.max(peak, axis=0, keepdims=True)
        total = jnp.sum(total * jnp.exp2(peak - best), axis=0, keepdims=True)
        for n in range(2):
            pair = unit[2 * n:2 * n + 2]
            rows_at = slice(n * lanes, (n + 1) * lanes)
            embs = quarters(values_of(pair), inv_e[rows_at, :])
            picked = picks[rows_at, :]
            inv = lax.rsqrt(jnp.sum(picked * picked, axis=1, keepdims=True) + 1e-06)
            picked = quarters(picked, inv)
            cosine = row_sum([u * p for u, p in zip(embs, picked)])
            across = [u - cosine * p for u, p in zip(embs, picked)]
            sine = jnp.sqrt(row_sum([v * v for v in across]))
            target = flip(cosine * COS_MARGIN - sine * SIN_MARGIN)[0:1, :]
            mine = local[:, rows_at]
            owned = (mine >= 0) & (mine < rows)
            tile = 2 * number + n
            stats[tile, 0:1, :] = best[:, rows_at]
            stats[tile, 1:2, :] = total[:, rows_at]
            stats[tile, 2:3, :] = jnp.where(owned, row_of(scale_ref, pair) * target, 0.0)

    def report(number, unit):
        for n, spot in enumerate(unit):
            _, block, p = where_of(spot)

            @pl.loop(0, piece // share)
            def _(t, tile=2 * number + n // 2, start=block * ncls + p * (piece // share)):
                to = start + t

                @pl.when(to != me)
                def _():
                    pltpu.make_async_remote_copy(
                        src_ref=stats.at[tile], dst_ref=got.at[me], send_sem=ss, recv_sem=sr,
                        device_id=(to // ncls, lax.rem(to, ncls)), device_id_type=MESH,
                    ).start()

    stats[:, 3:4, :] = jnp.zeros((2 * len(units), 1, lanes), jnp.float32)
    arrived = 0
    for number, unit in enumerate(units):
        while number >= 2 and arrived < 4 * (number - 1):
            d_copy(arrived).wait_recv()
            arrived += 1
        load_unit(unit)
        local = jnp.concatenate([row_of(lab_ref, unit[0:2]), row_of(lab_ref, unit[2:4])], axis=1) - offset
        below = local - ids
        carry = sweep(unit, below, number if 1 <= number <= 6 else None)
        if number == 0:
            forward(0)
        finish(number, unit, local, *carry)
        report(number, unit)

    got[me] = stats[2 + lax.rem(cls * share // piece, 4) // 2]
    for copy, plan in ((x_copy, x_plan), (y_copy, y_plan), (z_copy, z_plan), (d_copy, d_order)):
        for k in range(len(plan)):
            copy(k).wait_send()
    rest = got.at[pl.ds(0, ndev - 1)]
    pltpu.make_async_copy(rest, rest, ss).wait()
    pltpu.make_async_copy(rest, rest, sr).wait()

    peaks, totals = got[:, 0, :], got[:, 1, :]
    target = jnp.sum(got[:, 2, :], axis=0, keepdims=True)
    best = jnp.maximum(jnp.max(peaks, axis=0, keepdims=True), target * LOG2E)
    total = jnp.sum(totals * jnp.exp2(peaks - best), axis=0, keepdims=True) + jnp.exp2(target * LOG2E - best)
    loss = best * LN2 + jnp.log(total) - target
    per = lanes // share
    mine = loss[:, 0:share]
    for q in range(1, per):
        mine = jnp.where(lax.rem(me, per) == q, loss[:, q * share:(q + 1) * share], mine)
    out_ref[...] = mine


def body(embeddings, classifier, labels, row_scale):
    ndp, ncls = lax.axis_size("dp"), lax.axis_size("cls")
    assert ndp == 4 and ncls % 4 == 0
    ndev = ndp * ncls
    block, width = embeddings.shape
    rows = classifier.shape[0]
    count = labels.shape[0]
    lanes = block // 4
    chunk = rows // 8
    groups = count // lanes
    f32 = jnp.float32
    any_spec = pl.BlockSpec(memory_space=pl.ANY)
    vmem = pl.BlockSpec(memory_space=pltpu.VMEM)
    dma = pltpu.SemaphoreType.DMA
    out = pl.pallas_call(
        functools.partial(kernel, ndp, ncls, chunk),
        out_shape=jax.ShapeDtypeStruct((1, count // ndev), f32),
        in_specs=[any_spec, any_spec, pl.BlockSpec(memory_space=pltpu.SMEM), vmem, vmem],
        out_specs=vmem,
        scratch_shapes=[
            pltpu.VMEM((4, block, width), f32),
            pltpu.VMEM((rows, width), f32),
            pltpu.VMEM((rows, width), jnp.bfloat16),
            pltpu.VMEM((2 * lanes, width), f32),
            pltpu.VMEM((2 * lanes, width), jnp.bfloat16),
            pltpu.VMEM((2 * lanes, lanes), f32),
            pltpu.VMEM((16, 4, lanes), f32),
            pltpu.VMEM((ndev, 4, lanes), f32),
            dma, dma((8,)), dma((9,)), dma((9,)), dma((9,)), dma((9,)), dma((6,)), dma((6,)),
            dma((24,)), dma((24,)), dma, dma,
        ],
        compiler_params=pltpu.CompilerParams(
            collective_id=0, has_side_effects=True, vmem_limit_bytes=56 * 1024 * 1024
        ),
    )(embeddings, classifier, labels, labels.reshape(groups, lanes), row_scale.reshape(groups, lanes))
    return out.reshape(count // ndev)


def solution(mesh):
    placed = (P("dp", None), P(("dp", "cls"), None), P(), P())
    return jax.shard_map(
        body, mesh=mesh, in_specs=placed, out_specs=P(("dp", "cls")), check_vma=False
    )
```

time: 39.2 us -> 34.4 us (0.88)
  Pallas kernels: 37.7 us -> 33 us
    pallas_call x1, Pallas kernels: 37.7 us -> 33 us  [body(): pl.pallas_call(functools.partial(kernel, ndp, ncls, chunk), out_shape=jax...]
where the time goes in v2:
time: 34.4 us; the launch traced here: 34.2 us
  Pallas kernels  33 us (96%)
  local copies, waits for them, and re-layouts  1.19 us (3%)
    pallas_call x1, Pallas kernels, body(): pl.pallas_call(functools.partial(kernel, ndp, ncls, chunk), out_shape=jax...  33 us
    unnamed x1, local copies, waits for them, and re-layouts  1.19 us

profile of v2, /device:TPU:0, one launch (start us, length us, event | category | flops | bytes accessed | tf_op | source)
XLA Modules:
  0.0 34.2 jit_solution(12813122548720563447)
XLA Ops:
  0.0 33.0 %shard_map.46 = f32[1,64]{1,0:T(1,128)} custom-call(f32[512,512]{1,0:T(8,128)} %emb_hbm.1, f32[4096,512]{1,0:T(8,128)} %cls_hbm.1, s32[2048]{0:T(1024)} %lab_sm.1, s32[16,128]{1,0:T(8,128)} %bitcast.3, f32[16,128]{1,0:T(8,128)} %bitcast.4), custom_call_target="tpu_custom_call" | custom-call | tf_op jit(solution)/shard_map/pallas_call | solution.py:335
  33.0 1.2 %copy.6 = f32[64]{0:T(128)} copy(f32[64]{0:T(128)} %bitcast.5) | data formatting | bytes 512

commit v3 on v2

--- a/solution.py
+++ b/solution.py
@@ -26,7 +26,7 @@
 
 def kernel(ndp, ncls, chunk, emb_hbm, cls_hbm, lab_sm, lab_ref, scale_ref, out_ref,
            emb, raw, unit_w, picks, unit_e, inv_e, stats, got,
-           emb_sem, raw_sem, xs, xr, ys, yr, zs, zr, ds, dr, ss, sr):
+           emb_sem, raw_sem, xs, xr, ys, yr, zs, zr, ds, dr, ss, sr, rounds):
     dp, cls = lax.axis_index("dp"), lax.axis_index("cls")
     core = lax.rem(cls, 2)
     ndev = ndp * ncls
@@ -41,12 +41,27 @@
 
     emb_in = pltpu.make_async_copy(emb_hbm, emb.at[0], emb_sem)
     emb_in.start()
+    to_x = (dp ^ 1, cls)
+    to_y = (dp ^ 2, cls)
+    to_z = (dp, cls ^ 2)
+    partner = (dp, cls ^ 1)
+    has_low, has_high = cls >= 2, cls + 2 < ncls
+    beside = 3 + has_low.astype(jnp.int32) + has_high.astype(jnp.int32)
+
+    def greet(sem):
+        for to in (to_x, to_y, partner):
+            pl.semaphore_signal(sem, inc=1, device_id=to, device_id_type=MESH)
+
+        @pl.when(has_low)
+        def _():
+            pl.semaphore_signal(sem, inc=1, device_id=(dp, cls - 2), device_id_type=MESH)
+
+        @pl.when(has_high)
+        def _():
+            pl.semaphore_signal(sem, inc=1, device_id=(dp, cls + 2), device_id_type=MESH)
+
     barrier = pltpu.get_barrier_semaphore()
-
-    @pl.loop(1, ndev)
-    def _(k):
-        to = lax.rem(me + k, ndev)
-        pl.semaphore_signal(barrier, inc=1, device_id=(to // ncls, lax.rem(to, ncls)), device_id_type=MESH)
+    greet(barrier)
 
     raw_in = [
         pltpu.make_async_copy(cls_hbm.at[pl.ds(i * chunk, chunk)], raw.at[pl.ds(i * chunk, chunk)], raw_sem.at[i])
@@ -55,12 +70,15 @@
     for copy in raw_in:
         copy.start()
     emb_in.wait()
-    pl.semaphore_wait(barrier, ndev - 1)
-
-    to_x = (dp ^ 1, cls)
-    to_y = (dp ^ 2, cls)
-    to_z = (dp, cls ^ 2)
-    partner = (dp, cls ^ 1)
+    pl.semaphore_wait(barrier, beside)
+    last_round = ncls // 2
+    greet(rounds.at[0])
+
+    def hear(r):
+        pl.semaphore_wait(rounds.at[r], beside)
+        if r < last_round:
+            greet(rounds.at[r + 1])
+
     near = cls * share // (4 * piece) * 4
     starts = (4 - near, near)
     turn = lax.rem(cls // 2, 2) * 2
@@ -159,6 +177,7 @@
 
     for i in range(nchunk):
         prepare(i)
+    hear(0)
 
     zx, zy = sy, sx
     units = [
@@ -296,7 +315,15 @@
         if number == 0:
             forward(0)
         finish(number, unit, local, *carry)
-        report(number, unit)
+        if number < 3:
+            hear(number + 1)
+        elif number == 3:
+            for r in range(4, last_round + 1):
+                hear(r)
+            for k in range(4):
+                report(k, units[k])
+        else:
+            report(number, unit)
 
     got[me] = stats[2 + lax.rem(cls * share // piece, 4) // 2]
     for copy, plan in ((x_copy, x_plan), (y_copy, y_plan), (z_copy, z_plan), (d_copy, d_order)):
@@ -347,7 +374,7 @@
             pltpu.VMEM((16, 4, lanes), f32),
             pltpu.VMEM((ndev, 4, lanes), f32),
             dma, dma((8,)), dma((9,)), dma((9,)), dma((9,)), dma((9,)), dma((6,)), dma((6,)),
-            dma((24,)), dma((24,)), dma, dma,
+            dma((24,)), dma((24,)), dma, dma, pltpu.SemaphoreType.REGULAR((ncls // 2 + 1,)),
         ],
         compiler_params=pltpu.CompilerParams(
             collective_id=0, has_side_effects=True, vmem_limit_bytes=56 * 1024 * 1024

time: 34.4 us -> 32.4 us (0.942)
  Pallas kernels: 33 us -> 31 us
    pallas_call x1, Pallas kernels: 33 us -> 31 us  [body(): pl.pallas_call(functools.partial(kernel, ndp, ncls, chunk), out_shape=jax...]
where the time goes in v3:
time: 32.4 us; the launch traced here: 32.2 us
  Pallas kernels  31 us (96%)
  local copies, waits for them, and re-layouts  1.19 us (4%)
    pallas_call x1, Pallas kernels, body(): pl.pallas_call(functools.partial(kernel, ndp, ncls, chunk), out_shape=jax...  31 us
    unnamed x1, local copies, waits for them, and re-layouts  1.19 us

profile of v3, /device:TPU:0, one launch (start us, length us, event | category | flops | bytes accessed | tf_op | source)
XLA Modules:
  0.0 32.2 jit_solution(17944804336750257456)
XLA Ops:
  0.0 31.0 %shard_map.46 = f32[1,64]{1,0:T(1,128)} custom-call(f32[512,512]{1,0:T(8,128)} %emb_hbm.1, f32[4096,512]{1,0:T(8,128)} %cls_hbm.1, s32[2048]{0:T(1024)} %lab_sm.1, s32[16,128]{1,0:T(8,128)} %bitcast.3, f32[16,128]{1,0:T(8,128)} %bitcast.4), custom_call_target="tpu_custom_call" | custom-call | tf_op jit(solution)/shard_map/pallas_call | solution.py:362
  31.0 1.2 %copy.6 = f32[64]{0:T(128)} copy(f32[64]{0:T(128)} %bitcast.5) | data formatting | bytes 512

commit v4 on v3

--- a/solution.py
+++ b/solution.py
@@ -142,8 +142,8 @@
         [(*X, 2), (*Y, 2), (*X, 3), (*Y, 3)],
         [(*Z, 0), (*Z, 1), (*X, 4), (*Y, 4)],
         [(*Z, 2), (*X, 5), (*Y, 5), (*Z, 3)],
-        [(*X, 6), (*Y, 6), (*Z, 4), (*Z, 5)],
-        [(*X, 7), (*Y, 7), (*X, 8), (*Y, 8)],
+        [(*X, 6), (*Y, 6), (*Z, 4), (*Y, 7)],
+        [(*X, 7), (*X, 8), (*Y, 8), (*Z, 5)],
     ]
     relays = [
         [(z_copy, 0), (z_copy, 1)],
@@ -187,8 +187,8 @@
         [(1, N, sx), (1, N, at(sx, 1)), (2, N, sy), (2, N, at(sy, 1))],
         [(1, F, zx), (2, F, at(zy, 1)), (3, F, sy), (3, F, at(sx, 1))],
         [(3, F, sx), (3, F, at(sy, 1)), (2, F, zy), (1, F, at(zx, 1))],
-        [(2, N, sx), (1, N, at(sy, 1)), (1, N, zx), (2, N, at(zy, 1))],
-        [(3, N, sy), (3, N, at(sy, 1)), (3, N, sx), (3, N, at(sx, 1))],
+        [(2, N, sx), (1, N, at(sy, 1)), (1, N, zx), (3, N, at(sx, 1))],
+        [(3, N, sy), (3, N, at(sy, 1)), (3, N, sx), (2, N, at(zy, 1))],
     ]
     wide = 4 * piece
     tall = rows // 2
@@ -212,10 +212,10 @@
         for spot in pair:
             slot, _, p = where_of(spot)
             both.append(emb[slot, pl.ds(pl.multiple_of(p * piece, piece), piece), :])
-        return jnp.concatenate(both, axis=0)
+        return jnp.concatenate(both, axis=0) if len(both) > 1 else both[0]
 
     def quarters(values, factor):
-        return [values[:, q:q + lanes] * factor for q in range(0, width, lanes)]
+        return [values[:, q:q + lanes] if factor is None else values[:, q:q + lanes] * factor for q in range(0, width, lanes)]
 
     def row_sum(parts):
         return jnp.sum(tree(parts, jnp.add), axis=1, keepdims=True)
@@ -272,14 +272,18 @@
         for n in range(2):
             pair = unit[2 * n:2 * n + 2]
             rows_at = slice(n * lanes, (n + 1) * lanes)
-            embs = quarters(values_of(pair), inv_e[rows_at, :])
-            picked = picks[rows_at, :]
-            inv = lax.rsqrt(jnp.sum(picked * picked, axis=1, keepdims=True) + 1e-06)
-            picked = quarters(picked, inv)
-            cosine = row_sum([u * p for u, p in zip(embs, picked)])
-            across = [u - cosine * p for u, p in zip(embs, picked)]
-            sine = jnp.sqrt(row_sum([v * v for v in across]))
-            target = flip(cosine * COS_MARGIN - sine * SIN_MARGIN)[0:1, :]
+            columns = []
+            for h, spot in enumerate(pair):
+                part_at = slice(n * lanes + h * piece, n * lanes + (h + 1) * piece)
+                embs = quarters(values_of([spot]), inv_e[part_at, :])
+                picked = picks[part_at, :]
+                inv = lax.rsqrt(row_sum([v * v for v in quarters(picked, None)]) + 1e-06)
+                picked = quarters(picked, inv)
+                cosine = row_sum([u * p for u, p in zip(embs, picked)])
+                across = [u - cosine * p for u, p in zip(embs, picked)]
+                sine = jnp.sqrt(row_sum([v * v for v in across]))
+                columns.append(jnp.broadcast_to(cosine * COS_MARGIN - sine * SIN_MARGIN, (piece, lanes)))
+            target = jnp.transpose(jnp.concatenate(columns, axis=0))[0:1, :]
             mine = local[:, rows_at]
             owned = (mine >= 0) & (mine < rows)
             tile = 2 * number + n

time: 32.4 us -> 32.4 us (level)
  no operation moved by 1% of the time
where the time goes in v4:
time: 32.4 us; the launch traced here: 32.1 us
  Pallas kernels  30.9 us (95%)
  local copies, waits for them, and re-layouts  1.19 us (4%)
    pallas_call x1, Pallas kernels, body(): pl.pallas_call(functools.partial(kernel, ndp, ncls, chunk), out_shape=jax...  30.9 us
    unnamed x1, local copies, waits for them, and re-layouts  1.19 us

profile of v4, /device:TPU:0, one launch (start us, length us, event | category | flops | bytes accessed | tf_op | source)
XLA Modules:
  0.0 32.1 jit_solution(17037193042166143314)
XLA Ops:
  0.0 30.9 %shard_map.46 = f32[1,64]{1,0:T(1,128)} custom-call(f32[512,512]{1,0:T(8,128)} %emb_hbm.1, f32[4096,512]{1,0:T(8,128)} %cls_hbm.1, s32[2048]{0:T(1024)} %lab_sm.1, s32[16,128]{1,0:T(8,128)} %bitcast.3, f32[16,128]{1,0:T(8,128)} %bitcast.4), custom_call_target="tpu_custom_call" | custom-call | tf_op jit(solution)/shard_map/pallas_call | solution.py:366
  31.0 1.2 %copy.6 = f32[64]{0:T(128)} copy(f32[64]{0:T(128)} %bitcast.5) | data formatting | bytes 512
